TPU v7x, 32 devices: a whole 2x2x4 slice. The times are simulated.
32 devices in a mesh: groups: 2 (over y), kvb: 4 (over z), tp: 4 (over x, core).
Axes of the slice: x: 2, y: 2, z: 4, core: 2. Of those that a mesh axis runs over, the one named last changes fastest.
Arguments:
- residual: bfloat16 [32, 8192], P(('groups', 'kvb')), parts along dimension 0, may hold values from -3 to 3
- queries: bfloat16 [32, 8192], P(('groups', 'kvb'), 'tp'), parts along dimension 0, may hold values from -60 to 60
- new_kv: bfloat16 [32, 2048], P(('groups', 'kvb')), parts along dimension 0, may hold values from -6 to 6
- kv_cache: bfloat16 [2048, 16, 2048], P(('groups', 'kvb', 'tp')), parts along dimension 0, may hold values from -6 to 6
- lengths: int32 [32], P('groups'), parts along dimension 0, may hold values from 1 to 2048, as said below
- slot_seq: int32 [2048], P(('groups', 'kvb', 'tp')), parts along dimension 0, may hold values from 0 to 15, as said below
- slot_block: int32 [2048], P(('groups', 'kvb', 'tp')), parts along dimension 0, may hold values from 0 to 127, as said below
- block_counts: int32 [32], P(('groups', 'kvb', 'tp')), parts along dimension 0, may hold values from 16 to 64, as said below
- out_weight: bfloat16 [8192, 8192], P('tp'), may hold values from -0.5 to 0.5
- norm_gain: bfloat16 [8192], P('tp'), may hold values from 0.099609375 to 1.8984375
Outputs:
- stream: bfloat16 [32, 8192], P(('groups', 'kvb'), 'tp'), parts along dimension 0
- normed: bfloat16 [32, 8192], P(('groups', 'kvb'), 'tp'), parts along dimension 0
There are 2 independent parts, one for each index of `groups`. A program takes and returns all parts, laid end to end along the dimension named above; an argument that names none is the same for every part. Nothing has to cross between parts.
Inputs may be any that keep to these rules, and one draw needn't show every extreme that they name: `block_counts`: slots below a device's count hold cache blocks, those at or beyond it none; at least one device's count is 64. `slot_seq`: each pair of a sequence s and a block b below ceil(lengths[s] / 16) sits in exactly one live slot of the group. `slot_block`: some sequence has exactly 128 blocks; none has more. `lengths`: some sequence has exactly 16 * (128) tokens.
All inputs are finite; a program needn't handle non-finite values.
Results may differ from a plain program's by a relative error of at most 0.006.
Values may be sent and summed in bfloat16 or wider, within the bound.
No kernel may reach another device: no remote copies, remote signals or barrier semaphores. Data moves between devices by JAX's collectives and lax.ppermute only.
A program may use at most 64 MiB of HBM per device.

v0:
```python
import jax
import jax.numpy as jnp
from jax import lax
from jax.sharding import PartitionSpec as P

QH = 64
KVH = 8
HD = 128
BLK = 16


NEGATIVE = -1e30
EPSILON = 1e-06


def on_device(
    residual,
    queries,
    new_kv,
    kv_cache,
    lengths,
    slot_seq,
    slot_block,
    block_counts,
    out_weight,
    norm_gain,
):
    tp_count = lax.axis_size("tp")
    kvb_count = lax.axis_size("kvb")
    tp_index = lax.axis_index("tp")
    seq_rep = residual.shape[0]
    local_heads = queries.shape[1] // HD
    group_size = QH // KVH
    score_scale = HD ** (-0.5)
    wide = lax.all_gather(queries, "tp", axis=1, tiled=True)
    every = lax.all_gather(wide, "kvb", axis=0, tiled=True)
    seq_total = every.shape[0]
    grouped = every.reshape(seq_total, KVH, group_size, HD)
    pool_size = kv_cache.shape[0]
    step_slots = min(32, pool_size)
    live_count = block_counts[0]
    seq_ids = jnp.arange(seq_total, dtype=jnp.int32)
    offsets = jnp.arange(BLK, dtype=jnp.int32)

    def advance(turn_index, carried):
        peak_now, weight_sum, partial_rows = carried
        first_slot = turn_index * step_slots
        cache_part = lax.dynamic_slice_in_dim(kv_cache, first_slot, step_slots, 0)
        seq_part = lax.dynamic_slice_in_dim(slot_seq, first_slot, step_slots, 0)
        block_part = lax.dynamic_slice_in_dim(slot_block, first_slot, step_slots, 0)
        key_rows = cache_part[:, :, : KVH * HD].reshape(step_slots * BLK, KVH, HD)
        value_rows = cache_part[:, :, KVH * HD :].reshape(step_slots * BLK, KVH, HD)
        token_seq = jnp.repeat(seq_part, BLK)
        position = (block_part[:, None] * BLK + offsets[None, :]).reshape(-1)
        slot_live = jnp.repeat(
            first_slot + jnp.arange(step_slots, dtype=jnp.int32) < live_count, BLK
        )
        member = token_seq[None, :] == seq_ids[:, None]
        length_of = jnp.sum(jnp.where(member, lengths[:, None], 0), axis=0)
        live = member & (position < length_of)[None, :] & slot_live[None, :]
        mask = live[:, None, None, :]
        scores = (
            jnp.einsum("sgqd,ngd->sgqn", grouped, key_rows, preferred_element_type=jnp.float32)
            * score_scale
        )
        peak_next = jnp.maximum(peak_now, jnp.max(jnp.where(mask, scores, NEGATIVE), axis=-1))
        weights = jnp.where(mask, jnp.exp(scores - peak_next[..., None]), 0.0)
        shrink = jnp.exp(peak_now - peak_next)
        weight_sum = weight_sum * shrink + jnp.sum(weights, axis=-1)
        partial_rows = partial_rows * shrink[..., None] + jnp.einsum(
            "sgqn,ngd->sgqd",
            weights.astype(jnp.bfloat16),
            value_rows,
            preferred_element_type=jnp.float32,
        )
        return (peak_next, weight_sum, partial_rows)

    start_state = (
        jnp.full((seq_total, KVH, group_size), NEGATIVE, jnp.float32),
        jnp.zeros((seq_total, KVH, group_size), jnp.float32),
        jnp.zeros((seq_total, KVH, group_size, HD), jnp.float32),
    )
    turn_count = (live_count + step_slots - 1) // step_slots
    peak_now, weight_sum, partial_rows = lax.fori_loop(0, turn_count, advance, start_state)
    row_out = partial_rows.reshape(kvb_count, seq_rep, tp_count, local_heads * HD).transpose(
        0, 2, 1, 3
    )
    peak_out = peak_now.reshape(kvb_count, seq_rep, tp_count, local_heads).transpose(0, 2, 1, 3)
    sum_out = weight_sum.reshape(kvb_count, seq_rep, tp_count, local_heads).transpose(0, 2, 1, 3)
    device_total = kvb_count * tp_count
    got_rows, got_peaks, got_sums = (
        lax.all_to_all(
            row_out.reshape(device_total, seq_rep, local_heads * HD),
            ("kvb", "tp"),
            split_axis=0,
            concat_axis=0,
            tiled=True,
        ),
        lax.all_to_all(
            peak_out.reshape(device_total, seq_rep, local_heads),
            ("kvb", "tp"),
            split_axis=0,
            concat_axis=0,
            tiled=True,
        ),
        lax.all_to_all(
            sum_out.reshape(device_total, seq_rep, local_heads),
            ("kvb", "tp"),
            split_axis=0,
            concat_axis=0,
            tiled=True,
        ),
    )
    got_rows = got_rows.reshape(device_total, seq_rep, local_heads, HD)
    kv_local = max(1, local_heads // group_size)
    per_kv = local_heads // kv_local
    kv_first = tp_index * local_heads // group_size
    new_keys = lax.dynamic_slice_in_dim(new_kv, kv_first * HD, kv_local * HD, 1).reshape(
        seq_rep, kv_local, HD
    )
    new_values = lax.dynamic_slice_in_dim(new_kv, KVH * HD + kv_first * HD, kv_local * HD, 1)
    new_values = new_values.reshape(seq_rep, kv_local, 1, HD).astype(jnp.float32)
    own_view = queries.reshape(seq_rep, kv_local, per_kv, HD)
    fresh = (
        jnp.einsum("rkqd,rkd->rkq", own_view, new_keys, preferred_element_type=jnp.float32)
        * score_scale
    )
    fresh = fresh.reshape(seq_rep, local_heads)
    fresh_values = jnp.broadcast_to(new_values, (seq_rep, kv_local, per_kv, HD)).reshape(
        seq_rep, local_heads, HD
    )
    overall = jnp.maximum(jnp.max(got_peaks, axis=0), fresh)
    scaling = jnp.exp(got_peaks - overall[None])
    fresh_weight = jnp.exp(fresh - overall)
    denominator = jnp.sum(scaling * got_sums, axis=0) + fresh_weight
    numerator = (
        jnp.sum(scaling[..., None] * got_rows, axis=0) + fresh_weight[..., None] * fresh_values
    )
    attended = (
        (numerator / denominator[..., None]).reshape(seq_rep, local_heads * HD).astype(jnp.bfloat16)
    )
    projected = jnp.dot(attended, out_weight, preferred_element_type=jnp.float32)
    width_dev = norm_gain.shape[0]
    column = tp_index * width_dev
    summed = lax.psum(projected, "tp")
    full_stream = (residual.astype(jnp.float32) + summed).astype(jnp.bfloat16)
    full_wide = lax.optimization_barrier(full_stream).astype(jnp.float32)
    mean_square = jnp.mean(full_wide * full_wide, axis=1)
    stream = lax.dynamic_slice_in_dim(full_stream, column, width_dev, 1)
    stream_wide = lax.dynamic_slice_in_dim(full_wide, column, width_dev, 1)
    normed = (
        stream_wide * lax.rsqrt(mean_square + EPSILON)[:, None] * norm_gain.astype(jnp.float32)
    ).astype(jnp.bfloat16)
    return (stream, normed)


def solution(mesh):
    placed = (
        P(("groups", "kvb"), None),
        P(("groups", "kvb"), "tp"),
        P(("groups", "kvb"), None),
        P(("groups", "kvb", "tp"), None, None),
        P("groups"),
        P(("groups", "kvb", "tp")),
        P(("groups", "kvb", "tp")),
        P(("groups", "kvb", "tp")),
        P("tp", None),
        P("tp"),
    )
    return jax.shard_map(
        on_device,
        mesh=mesh,
        in_specs=placed,
        out_specs=(P(("groups", "kvb"), "tp"), P(("groups", "kvb"), "tp")),
        check_vma=False,
    )
```

profile of v0, /device:TPU:0, one launch (start us, length us, event | category | flops | bytes accessed | tf_op | source)
XLA Modules:
  0.0 140.4 jit_solution(4578274907591061050)
XLA Ops:
  7.8 6.5 %all_gather.6 = bf16[4,8192]{1,0:T(4,128)(2,1)S(1)} all-gather(bf16[4,2048]{1,0:T(4,128)(2,1)} %param.13), channel_id=1, replica_groups=mesh['groups'=2,'kvb'=4,'tp'=4] {'tp'}, dimensions={1}, use_global_device_ids=true | all-gather | bytes 81920 | tf_op jit(solution)/shard_map/all_gather | solution.py:35
  14.3 14.5 %all-gather = bf16[4,4,8192]{2,1,0:T(4,128)(2,1)S(1)} all-gather(bf16[1,4,8192]{2,1,0:T(4,128)(2,1)S(1)} %bitcast.100), channel_id=1, replica_groups=mesh['groups'=2,'kvb'=4,'tp'=4] {'kvb'}, dimensions={0}, use_global_device_ids=true | all-gather | bytes 327680 | tf_op jit(solution)/shard_map/all_gather | solution.py:36
  28.8 0.3 reshape.180
  29.1 0.2 copy.33
  29.4 0.0 copy-start.1
  29.4 7.9 %while.17 = (s32[]{:T(128)}, f32[16,8,8]{0,2,1:T(8,128)S(1)}, f32[16,8,8]{0,2,1:T(8,128)S(1)}, f32[16,8,8,128]{3,0,2,1:T(8,128)S(1)}, s32[]{:T(128)}, /*index=5*...) while((s32[]{:T(128)}, f32[16,8,8]{0,2,1:T(8,128)S(1)}, ...), condition=%wide.region_4.5_spmd.clone.clone, body=%wide.region_0.4_spmd.clone.clone.sunk | while | flops 274516576 | bytes 18212968 | solution.py:84
  29.4 0.7 dynamic_slice.42
  30.2 0.1 broadcast_in_dim.134
  30.2 0.1 eq.54
  30.3 0.7 fusion.44
  31.1 0.7 dynamic-slice_multiply_fusion.2
  31.8 0.1 iota_add_fusion.2
  31.9 0.1 add.156
  32.0 0.7 add_compare_fusion.2
  32.6 0.1 broadcast_in_dim.135
  32.7 0.1 and.71
  32.8 1.7 %constant_dynamic-slice_fusion.5 = (bf16[32,16,1024]{2,1,0:T(8,128)(2,1)S(1)}, bf16[32,16,1024]{2,1,0:T(8,128)(2,1)S(1)}) fusion(bf16[64,16,2048]{2,1,0:T(8,128)(2,1)} %get-tuple-element.348, s32[]{:T(128)S(6)} %select_n.72, s32[]{:T(128)S(6)} %add.157), kind=kLoop, calls=%fused_computation.28.clone.1 | loop fusion | bytes 4194312 | tf_op jit(solution)/shard_map/while/body/slice | solution.py:52
  34.5 0.3 copy.84
  34.8 0.6 fusion.46
  35.4 0.6 fusion.47
  36.1 0.3 copy.85
  36.3 0.9 fusion.48
  37.3 0.1 copy.34
  37.4 0.1 reshape.181
  37.5 0.6 copy.36
  38.1 13.2 %all-to-all-start = ((f32[16,4,16]{2,1,0:T(4,128)}), f32[16,4,16]{2,1,0:T(4,128)S(1)}, u32[]{:S(2)}, u32[]{:S(2)}) async-start(f32[16,4,16]{2,1,0:T(4,128)} %copy.36), calls=%async_computation | async-start | bytes 65536 | tf_op jit(solution)/shard_map/all_to_all | solution.py:99
  51.4 0.7 dynamic-slice_convert_fusion
  52.1 0.1 copy.39
  52.2 0.1 reshape.189
  52.3 0.6 copy.41
  52.9 5.1 %all-to-all-done = f32[16,4,16]{2,1,0:T(4,128)S(1)} async-done(((f32[16,4,16]{2,1,0:T(4,128)}), f32[16,4,16]{2,1,0:T(4,128)S(1)}, u32[]{:S(2)}, u32[]{:S(2)}) %all-to-all-start) | async-done | bytes 4128 | tf_op jit(solution)/shard_map/all_to_all | solution.py:99
  58.0 3.5 %all-to-all-start.2 = ((f32[16,4,16]{2,1,0:T(4,128)}), f32[16,4,16]{2,1,0:T(4,128)S(1)}, u32[]{:S(2)}, u32[]{:S(2)}) async-start(f32[16,4,16]{2,1,0:T(4,128)} %copy.41), calls=%async_computation.2 | async-start | bytes 65536 | tf_op jit(solution)/shard_map/all_to_all | solution.py:106
  61.5 0.0 copy-done.1
  61.5 0.1 fusion.26
  61.6 0.2 copy.37
  61.8 0.2 reshape.186
  62.0 1.1 copy.38
  63.1 5.0 %all-to-all-done.2 = f32[16,4,16]{2,1,0:T(4,128)S(1)} async-done(((f32[16,4,16]{2,1,0:T(4,128)}), f32[16,4,16]{2,1,0:T(4,128)S(1)}, u32[]{:S(2)}, u32[]{:S(2)}) %all-to-all-start.2) | async-done | bytes 4128 | tf_op jit(solution)/shard_map/all_to_all | solution.py:106
  68.1 3.6 %all-to-all-start.1 = ((f32[16,4,2048]{2,1,0:T(4,128)}), f32[16,4,2048]{2,1,0:T(4,128)S(1)}, u32[]{:S(2)}, u32[]{:S(2)}) async-start(f32[16,4,2048]{2,1,0:T(4,128)} %bitcast.7), calls=%async_computation.1 | async-start | bytes 1048576 | tf_op jit(solution)/shard_map/all_to_all | solution.py:92
  71.7 0.0 all-reduce.2.cloned.1.call-start
  71.7 0.1 reshape.185
  71.9 0.2 mul.96
  72.1 0.2 mul.97
  72.3 0.1 broadcast_bitcast_fusion
  72.4 13.5 %all-to-all-done.1 = f32[16,4,2048]{2,1,0:T(4,128)S(1)} async-done(((f32[16,4,2048]{2,1,0:T(4,128)}), f32[16,4,2048]{2,1,0:T(4,128)S(1)}, u32[]{:S(2)}, u32[]{:S(2)}) %all-to-all-start.1) | async-done | bytes 524320 | tf_op jit(solution)/shard_map/all_to_all | solution.py:92
  85.9 0.1 multiply_reduce_fusion
  86.1 0.0 copy-start.2
  86.1 0.0 copy-start
  86.1 13.5 %fusion.24 = f32[4,8192]{1,0:T(4,128)} fusion(bf16[2048,8192]{1,0:T(8,128)(2,1)} %param.20, f32[1,4,16,128]{3,2,1,0:T(8,128)S(1)} %get-tuple-element.225, f32[4,2048]{1,0:T(4,128)S(1)} %multiply_reduce_fusion, f32[1,4,16,128]{3,2,1,0:T(8,128)S(1)} %broadcast_bitcast_fusion.1, f32[1,4,16,128]{3,2,1,0:T(8,128)S(1)} %get-tuple-element.226), kind=kOutput, calls=%fused_computation.41 | convolution fusion | flops 134250496 | bytes 33816576 | tf_op jit(solution)/shard_map/dot_general | solution.py:142
  99.6 0.0 all-reduce.2.cloned.1.call-update
  99.6 0.0 copy-done.2
  99.6 31.4 %all-reduce.2.cloned.1.call-done = f32[4,8192]{1,0:T(4,128)} async-done(((f32[4,8192]{1,0:T(4,128)}), f32[4,8192]{1,0:T(4,128)}) %all-reduce.2.cloned.1.call-update) | async-done | bytes 131088 | tf_op jit(solution)/shard_map/psum | solution.py:145
  131.0 0.0 copy-done
  131.0 0.9 add_convert_fusion
  132.0 0.2 multiply_reduce_fusion.1
  132.2 0.6 constant_dynamic-slice_fusion.2
  132.8 0.7 multiply_convert_fusion
  (21 shorter events, 0.3 us)
Async XLA Ops:
  29.4 32.1 %copy-start.1 = (bf16[4,2048]{1,0:T(4,128)(2,1)S(1)}, bf16[4,2048]{1,0:T(4,128)(2,1)}, u32[]{:S(2)}) copy-start(bf16[4,2048]{1,0:T(4,128)(2,1)} %param.13) | copy-start | bytes 49156
  38.1 19.9 %all-to-all-start = ((f32[16,4,16]{2,1,0:T(4,128)}), f32[16,4,16]{2,1,0:T(4,128)S(1)}, u32[]{:S(2)}, u32[]{:S(2)}) async-start(f32[16,4,16]{2,1,0:T(4,128)} %copy.36), calls=%async_computation | async-start | bytes 65536 | tf_op jit(solution)/shard_map/all_to_all | solution.py:99
  58.0 10.1 %all-to-all-start.2 = ((f32[16,4,16]{2,1,0:T(4,128)}), f32[16,4,16]{2,1,0:T(4,128)S(1)}, u32[]{:S(2)}, u32[]{:S(2)}) async-start(f32[16,4,16]{2,1,0:T(4,128)} %copy.41), calls=%async_computation.2 | async-start | bytes 65536 | tf_op jit(solution)/shard_map/all_to_all | solution.py:106
  68.1 17.8 %all-to-all-start.1 = ((f32[16,4,2048]{2,1,0:T(4,128)}), f32[16,4,2048]{2,1,0:T(4,128)S(1)}, u32[]{:S(2)}, u32[]{:S(2)}) async-start(f32[16,4,2048]{2,1,0:T(4,128)} %bitcast.7), calls=%async_computation.1 | async-start | bytes 1048576 | tf_op jit(solution)/shard_map/all_to_all | solution.py:92
  71.7 59.4 %all-reduce.2.cloned.1.call-start = ((), (), s32[]{:S(2)}) async-start(), calls=%async_computation.3 | async-start | bytes 262144 | tf_op jit(solution)/shard_map/psum | solution.py:145
  86.1 13.6 %copy-start.2 = (bf16[2048]{0:T(1024)(128)(2,1)S(1)}, bf16[2048]{0:T(1024)(128)(2,1)}, u32[]{:S(2)}) copy-start(bf16[2048]{0:T(1024)(128)(2,1)} %param.21) | copy-start | bytes 12292
  86.1 45.0 %copy-start = (bf16[4,8192]{1,0:T(4,128)(2,1)S(1)}, bf16[4,8192]{1,0:T(4,128)(2,1)}, u32[]{:S(2)}) copy-start(bf16[4,8192]{1,0:T(4,128)(2,1)} %param.12) | copy-start | bytes 196612
Sparse Core Ops, SparseCore 0:
  99.7 31.2 all-reduce.1
where the time goes:
time: 141 us; the launch traced here: 140 us
  waiting for transfers between devices  55 us (39%)
  blocking collectives  21 us (15%)
  starting transfers between devices  20.4 us (14%)
  matrix products  15.1 us (11%)
  between operations  14.9 us (11%)
  local copies, waits for them, and re-layouts  8.16 us (6%)
  other arithmetic  5.66 us (4%)
    psum x1, waiting for transfers between devices, on_device(): summed = lax.psum(projected, 'tp')  31.4 us
    all_gather x1, blocking collectives, on_device(): every = lax.all_gather(wide, 'kvb', axis=0, tiled=True)  14.5 us
    dot_general x1, matrix products, on_device(): jnp.dot(attended, out_weight, preferred_element_type=jnp.float32)  13.5 us
    all_to_all x1, waiting for transfers between devices, on_device(): lax.all_to_all(row_out.reshape(device_total, seq_rep, local_heads * HD),...  13.5 us
    all_to_all x1, starting transfers between devices, on_device(): lax.all_to_all(peak_out.reshape(device_total, seq_rep, local_heads), ('kv...  13.2 us
    all_gather x1, blocking collectives, on_device(): wide = lax.all_gather(queries, 'tp', axis=1, tiled=True)  6.46 us
    all_to_all x1, waiting for transfers between devices, on_device(): lax.all_to_all(peak_out.reshape(device_total, seq_rep, local_heads), ('kv...  5.08 us
    all_to_all x1, waiting for transfers between devices, on_device(): lax.all_to_all(sum_out.reshape(device_total, seq_rep, local_heads), ('kvb...  4.97 us
  transfers between devices with their start and end apart: 4, of which 4 were waited for; matrix products, arithmetic and copies ran while one was open for 3% of the time, Pallas kernels for 0%

commit v1 on v0

v1 whole, which is shorter than its diff:
```python
import jax
import jax.numpy as jnp
from jax import lax
from jax.experimental import pallas as pl
from jax.experimental.pallas import tpu as pltpu
from jax.sharding import PartitionSpec as P

QH = 64
KVH = 8
HD = 128
BLK = 16

MASKED = -1e30
FLOOR = -1e20
EPSILON = 1e-06
UNIT = HD ** (-0.5) * 1.4426950408889634
STATS = 128


def attend_body(
    lengths, count, slot_seq, slot_block, wide, cache, out, stacked, *, kvb_count, tp_count
):
    slots = cache.shape[0]
    tokens = slots * BLK
    seq_rep = wide.shape[1]
    seq_total = kvb_count * seq_rep
    local_heads = wide.shape[2] // HD
    group_size = QH // KVH
    seq = slot_seq[...]
    length_of = jnp.zeros_like(seq)
    for s in range(seq_total):
        length_of = jnp.where(seq == s, lengths[s], length_of)
    slot_ids = lax.broadcasted_iota(jnp.int32, seq.shape, 1)
    remaining = jnp.clip(length_of - slot_block[...] * BLK, 0, BLK)
    remaining = jnp.where(slot_ids < count[0], remaining, 0)
    row = lax.broadcasted_iota(jnp.int32, (8, slots), 0)
    codes = jnp.where(row == 0, seq, jnp.where(row == 1, remaining, 0))
    spread = (
        lax.broadcasted_iota(jnp.int32, (slots, tokens), 1) // BLK
        == lax.broadcasted_iota(jnp.int32, (slots, tokens), 0)
    )
    per_token = jnp.dot(
        codes.astype(jnp.float32).astype(jnp.bfloat16),
        jnp.where(spread, 1.0, 0.0).astype(jnp.bfloat16),
        preferred_element_type=jnp.float32,
    )
    seq_ids = lax.broadcasted_iota(jnp.int32, (seq_total, tokens), 0).astype(jnp.float32)
    offsets = (lax.broadcasted_iota(jnp.int32, (seq_total, tokens), 1) % BLK).astype(jnp.float32)
    live = (per_token[0:1] == seq_ids) & (offsets < per_token[1:2])
    bias = jnp.where(live, 0.0, MASKED)

    for k in range(kvb_count):
        for t in range(tp_count):
            stacked[t, k * seq_rep : (k + 1) * seq_rep, :] = wide[k * tp_count + t].astype(
                jnp.float32
            )

    lane = lax.broadcasted_iota(jnp.int32, (seq_total, STATS), 1)
    stats = [jnp.zeros((seq_total, STATS), jnp.float32) for _ in range(tp_count)]
    for g in range(KVH):
        heads = [divmod(g * group_size + j, local_heads) for j in range(group_size)]
        rows = jnp.concatenate(
            [stacked[t, :, h * HD : (h + 1) * HD] for t, h in heads], axis=0
        ).astype(jnp.bfloat16)
        keys = cache[:, :, g * HD : (g + 1) * HD].reshape(tokens, HD)
        values = cache[:, :, (KVH + g) * HD : (KVH + g + 1) * HD].reshape(tokens, HD)
        scores = lax.dot_general(
            rows, keys, (((1,), (1,)), ((), ())), preferred_element_type=jnp.float32
        )
        scores = scores.reshape(group_size, seq_total, tokens) * UNIT + bias[None]
        peaks = jnp.maximum(jnp.max(scores, axis=2, keepdims=True), FLOOR)
        peaks = peaks.astype(jnp.bfloat16).astype(jnp.float32)
        weights = jnp.exp2(scores - peaks)
        sums = jnp.sum(weights, axis=2, keepdims=True)
        partial = jnp.dot(
            weights.astype(jnp.bfloat16).reshape(group_size * seq_total, tokens),
            values,
            preferred_element_type=jnp.float32,
        )
        high = sums.astype(jnp.bfloat16).astype(jnp.float32)
        low = sums - high
        for j, (t, h) in enumerate(heads):
            mine = partial[j * seq_total : (j + 1) * seq_total]
            for k in range(kvb_count):
                out[k * tp_count + t, :, h * HD : (h + 1) * HD] = mine[
                    k * seq_rep : (k + 1) * seq_rep
                ].astype(jnp.bfloat16)
            for part, value in enumerate((peaks, high, low)):
                stats[t] = jnp.where(lane == part * local_heads + h, value[j], stats[t])
    for t in range(tp_count):
        for k in range(kvb_count):
            out[k * tp_count + t, :, local_heads * HD :] = stats[t][
                k * seq_rep : (k + 1) * seq_rep
            ].astype(jnp.bfloat16)


def project_body(tp_index, got, queries, new_kv, weight, out, *, local_heads):
    sources, seq_rep, _ = got.shape
    group_size = QH // KVH
    width = local_heads * HD
    kv_local = max(1, local_heads // group_size)
    kv_first = tp_index[0] * local_heads // group_size
    lane = lax.broadcasted_iota(jnp.int32, (seq_rep, local_heads), 1)
    fresh = jnp.zeros((seq_rep, local_heads), jnp.float32)
    fresh_values = []
    for v in range(kv_local):
        at = pl.multiple_of((kv_first + v) * HD, HD)
        key = new_kv[:, pl.ds(at, HD)].astype(jnp.float32)
        at = pl.multiple_of((KVH + kv_first + v) * HD, HD)
        fresh_values.append(new_kv[:, pl.ds(at, HD)].astype(jnp.float32))
        for h in range(v * local_heads // kv_local, (v + 1) * local_heads // kv_local):
            query = queries[:, h * HD : (h + 1) * HD].astype(jnp.float32)
            score = jnp.sum(query * key, axis=1, keepdims=True)
            fresh = jnp.where(lane == h, score, fresh)
    fresh = fresh * UNIT
    peaks, sums = [], []
    overall = fresh
    for d in range(sources):
        stats = got[d, :, width:].astype(jnp.float32)
        peaks.append(stats[:, :local_heads])
        sums.append(
            stats[:, local_heads : 2 * local_heads] + stats[:, 2 * local_heads : 3 * local_heads]
        )
        overall = jnp.maximum(overall, peaks[-1])
    scaling = [jnp.exp2(p - overall) for p in peaks]
    fresh_weight = jnp.exp2(fresh - overall)
    denominator = fresh_weight
    for d in range(sources):
        denominator = denominator + scaling[d] * sums[d]
    inverse = 1.0 / denominator
    scaling = [s * inverse for s in scaling]
    fresh_weight = fresh_weight * inverse
    attended = []
    for h in range(local_heads):
        total = fresh_weight[:, h : h + 1] * fresh_values[h * kv_local // local_heads]
        for d in range(sources):
            total = total + scaling[d][:, h : h + 1] * got[d, :, h * HD : (h + 1) * HD].astype(
                jnp.float32
            )
        attended.append(total.astype(jnp.bfloat16))
    attended = jnp.concatenate(attended, axis=1)
    step = min(1024, weight.shape[1])
    for n in range(weight.shape[1] // step):
        out[:, n * step : (n + 1) * step] = jnp.dot(
            attended, weight[:, n * step : (n + 1) * step], preferred_element_type=jnp.float32
        ).astype(out.dtype)


def finish_body(tp_index, pieces, residual, gain, stream_out, normed_out):
    full = residual[...].astype(jnp.float32)
    width = full.shape[1]
    total = pieces[0].astype(jnp.float32)
    for t in range(1, pieces.shape[0]):
        total = total + pieces[t].astype(jnp.float32)
    full = (full + total).astype(jnp.bfloat16).astype(jnp.float32)
    mean_square = jnp.sum(full * full, axis=1, keepdims=True) / width
    inverse = lax.rsqrt(mean_square + EPSILON)
    own = stream_out.shape[1]
    at = pl.multiple_of(tp_index[0] * own, own)
    mine = residual[:, pl.ds(at, own)].astype(jnp.float32)
    total = pieces[0, :, pl.ds(at, own)].astype(jnp.float32)
    for t in range(1, pieces.shape[0]):
        total = total + pieces[t, :, pl.ds(at, own)].astype(jnp.float32)
    stream = (mine + total).astype(jnp.bfloat16)
    stream_out[...] = stream
    normed_out[...] = (stream.astype(jnp.float32) * inverse * gain[...].astype(jnp.float32)).astype(
        jnp.bfloat16
    )


def vmem():
    return pl.BlockSpec(memory_space=pltpu.VMEM)


def smem():
    return pl.BlockSpec(memory_space=pltpu.SMEM)


def on_device(
    residual,
    queries,
    new_kv,
    kv_cache,
    lengths,
    slot_seq,
    slot_block,
    block_counts,
    out_weight,
    norm_gain,
):
    tp_count = lax.axis_size("tp")
    kvb_count = lax.axis_size("kvb")
    device_total = kvb_count * tp_count
    tp_index = lax.axis_index("tp").reshape(1)
    seq_rep, own_width = queries.shape
    local_heads = own_width // HD
    seq_total = kvb_count * seq_rep
    wide = lax.all_to_all(
        jnp.broadcast_to(queries[None], (device_total, seq_rep, own_width)),
        ("kvb", "tp"),
        split_axis=0,
        concat_axis=0,
        tiled=True,
    )
    sent = pl.pallas_call(
        lambda *refs: attend_body(*refs, kvb_count=kvb_count, tp_count=tp_count),
        out_shape=jax.ShapeDtypeStruct((device_total, seq_rep, own_width + STATS), jnp.bfloat16),
        in_specs=[smem(), smem(), vmem(), vmem(), vmem(), vmem()],
        out_specs=vmem(),
        scratch_shapes=[pltpu.VMEM((tp_count, seq_total, own_width), jnp.float32)],
        compiler_params=pltpu.CompilerParams(vmem_limit_bytes=16 << 20),
        name="attend",
    )(lengths, block_counts, slot_seq[None], slot_block[None], wide, kv_cache)
    got = lax.all_to_all(sent, ("kvb", "tp"), split_axis=0, concat_axis=0, tiled=True)
    projected = pl.pallas_call(
        lambda *refs: project_body(*refs, local_heads=local_heads),
        out_shape=jax.ShapeDtypeStruct((seq_rep, out_weight.shape[1]), jnp.bfloat16),
        in_specs=[smem(), vmem(), vmem(), vmem(), vmem()],
        out_specs=vmem(),
        compiler_params=pltpu.CompilerParams(vmem_limit_bytes=48 << 20),
        name="project",
    )(tp_index, got, queries, new_kv, out_weight)
    pieces = lax.all_gather(projected, "tp", axis=0, tiled=False)
    own = jax.ShapeDtypeStruct((seq_rep, norm_gain.shape[0]), jnp.bfloat16)
    return pl.pallas_call(
        finish_body,
        out_shape=(own, own),
        in_specs=[smem(), vmem(), vmem(), vmem()],
        out_specs=(vmem(), vmem()),
        compiler_params=pltpu.CompilerParams(vmem_limit_bytes=8 << 20),
        name="finish",
    )(tp_index, pieces, residual, norm_gain[None])


def solution(mesh):
    placed = (
        P(("groups", "kvb"), None),
        P(("groups", "kvb"), "tp"),
        P(("groups", "kvb"), None),
        P(("groups", "kvb", "tp"), None, None),
        P("groups"),
        P(("groups", "kvb", "tp")),
        P(("groups", "kvb", "tp")),
        P(("groups", "kvb", "tp")),
        P("tp", None),
        P("tp"),
    )
    return jax.shard_map(
        on_device,
        mesh=mesh,
        in_specs=placed,
        out_specs=(P(("groups", "kvb"), "tp"), P(("groups", "kvb"), "tp")),
        check_vma=False,
    )
```

time: 141 us -> 66 us (0.47)
  waiting for transfers between devices: 55 us -> 18.9 us
  Pallas kernels: 0 us -> 20.6 us
  blocking collectives: 21 us -> 5.77 us
  matrix products: 15.1 us -> 0 us
  between operations: 14.9 us -> 1.31 us
  starting transfers between devices: 20.4 us -> 10.9 us
  other arithmetic: 5.66 us -> 0 us
    psum x1 -> x0, waiting for transfers between devices: 31.4 us -> none  [on_device(): summed = lax.psum(projected, 'tp')]
    pallas_call x0 -> x3, Pallas kernels: none -> 20.6 us  [the longest x1 15.4 us: on_device(): pl.pallas_call(lambda *refs: project_body(*refs, local_heads=local_heads)...]
    all_gather x2 -> x1, blocking collectives: 21 us -> 5.77 us  [on_device(): pieces = lax.all_gather(projected, 'tp', axis=0, tiled=False)]
    dot_general x4 -> x0, matrix products: 15.1 us -> none  [the longest x1 13.5 us: on_device(): jnp.dot(attended, out_weight, preferred_element_type=jnp.float32)]
    all_to_all x3 -> x2, starting transfers between devices: 20.3 us -> 10.9 us  [the longest x1 7.39 us: on_device(): lax.all_to_all(jnp.broadcast_to(queries[None], (device_total, seq_rep, ow...]
    unnamed x9 -> x14, local copies, waits for them, and re-layouts: 0.27 us -> 5.59 us
    all_to_all x3 -> x2, waiting for transfers between devices: 23.6 us -> 18.9 us  [the longest x1 9.54 us: on_device(): lax.all_to_all(sent, ('kvb', 'tp'), split_axis=0, concat_axis=0, tiled=True)]
    convert_element_type x5 -> x0, other arithmetic: 2.35 us -> none  [the longest x1 0.94 us: on_device(): full_stream = (residual.astype(jnp.float32) + summed).astype(jnp.bfloat16)]
  transfers between devices with their start and end apart: 4 -> 2, of which waited for: 4 -> 2; matrix products, arithmetic and copies ran while one was open for 3% -> 1% of each run, Pallas kernels for 0% -> 0%
where the time goes in v1:
time: 66 us; the launch traced here: 65.4 us
  Pallas kernels  20.6 us (31%)
  waiting for transfers between devices  18.9 us (29%)
  starting transfers between devices  10.9 us (17%)
  local copies, waits for them, and re-layouts  7.85 us (12%)
  blocking collectives  5.77 us (9%)
  between operations  1.31 us (2%)
    pallas_call x1, Pallas kernels, on_device(): pl.pallas_call(lambda *refs: project_body(*refs, local_heads=local_heads)...  15.4 us
    all_to_all x1, waiting for transfers between devices, on_device(): lax.all_to_all(sent, ('kvb', 'tp'), split_axis=0, concat_axis=0, tiled=True)  9.54 us
    all_to_all x1, waiting for transfers between devices, on_device(): lax.all_to_all(jnp.broadcast_to(queries[None], (device_total, seq_rep, ow...  9.37 us
    all_to_all x1, starting transfers between devices, on_device(): lax.all_to_all(jnp.broadcast_to(queries[None], (device_total, seq_rep, ow...  7.39 us
    all_gather x1, blocking collectives, on_device(): pieces = lax.all_gather(projected, 'tp', axis=0, tiled=False)  5.77 us
    unnamed x14, local copies, waits for them, and re-layouts  5.59 us
    pallas_call x1, Pallas kernels, on_device(): pl.pallas_call(lambda *refs: attend_body(*refs, kvb_count=kvb_count, tp_c...  4.39 us
    all_to_all x1, starting transfers between devices, on_device(): lax.all_to_all(sent, ('kvb', 'tp'), split_axis=0, concat_axis=0, tiled=True)  3.53 us
  transfers between devices with their start and end apart: 2, of which 2 were waited for; matrix products, arithmetic and copies ran while one was open for 1% of the time, Pallas kernels for 0%

profile of v1, /device:TPU:0, one launch (start us, length us, event | category | flops | bytes accessed | tf_op | source)
XLA Modules:
  0.0 65.4 jit_solution(10922960643431746860)
XLA Ops:
  0.6 0.0 copy-start.2
  0.6 1.6 %broadcast_in_dim.17 = bf16[16,4,2048]{2,1,0:T(4,128)(2,1)} broadcast(bf16[4,2048]{1,0:T(4,128)(2,1)} %refs_2_.1), dimensions={1,2} | broadcast | bytes 278528 | tf_op jit(solution)/shard_map/broadcast_in_dim | solution.py:199
  2.2 7.4 %all-to-all-start = ((bf16[16,4,2048]{2,1,0:T(4,128)(2,1)}), bf16[16,4,2048]{2,1,0:T(4,128)(2,1)S(1)}, u32[]{:S(2)}, u32[]{:S(2)}) async-start(bf16[16,4,2048]{2,1,0:T(4,128)(2,1)} %broadcast_in_dim.17), calls=%async_computation | async-start | bytes 524288 | tf_op jit(solution)/shard_map/all_to_all | solution.py:198
  10.2 9.4 %all-to-all-done.refs_4_ = bf16[16,4,2048]{2,1,0:T(4,128)(2,1)S(1)} async-done(((bf16[16,4,2048]{2,1,0:T(4,128)(2,1)}), bf16[16,4,2048]{2,1,0:T(4,128)(2,1)S(1)}, u32[]{:S(2)}, u32[]{:S(2)}) %all-to-all-start) | async-done | bytes 262176 | tf_op jit(solution)/shard_map/all_to_all | solution.py:198
  19.6 0.0 copy-start
  19.6 2.2 %copy-done = bf16[64,16,2048]{2,1,0:T(8,128)(2,1)S(1)} copy-done((bf16[64,16,2048]{2,1,0:T(8,128)(2,1)S(1)}, bf16[64,16,2048]{2,1,0:T(8,128)(2,1)}, u32[]{:S(2)}) %copy-start) | copy-done | bytes 4194328
  21.8 0.0 copy-start.4
  21.8 0.7 copy-done.4
  22.5 0.0 copy-start.5
  22.5 0.7 copy-done.5
  23.1 0.0 copy-start.6
  23.1 0.7 copy-done.6
  23.8 4.4 %attend.1 = bf16[16,4,2176]{2,1,0:T(4,128)(2,1)} custom-call(s32[16]{0:T(128)S(1)} %copy-done.4, s32[1]{0:T(128)S(6)} %copy.12.refs_1_, s32[1,64]{1,0:T(1,128)S(1)} %bitcast.5, s32[1,64]{1,0:T(1,128)S(1)} %bitcast.6, bf16[16,4,2048]{2,1,0:T(4,128)(2,1)S(1)} %all-to-all-done.refs_4_, bf16[64,16,2048]{2,1,0:T(8,128)(2,1)S(1)} %copy-done), custom_call_target="tpu_custom_call" | custom-call | tf_op jit(solution)/shard_map/attend/pallas_call | solution.py:205
  28.2 3.5 %all-to-all-start.1 = ((bf16[16,4,2176]{2,1,0:T(4,128)(2,1)}), bf16[16,4,2176]{2,1,0:T(4,128)(2,1)S(1)}, u32[]{:S(2)}, u32[]{:S(2)}) async-start(bf16[16,4,2176]{2,1,0:T(4,128)(2,1)} %attend.1), calls=%async_computation.1 | async-start | bytes 557056 | tf_op jit(solution)/shard_map/all_to_all | solution.py:214
  31.7 0.7 %broadcast_in_dim.18.gain = bf16[1,2048]{1,0:T(2,128)(2,1)S(1)} reshape(bf16[2048]{0:T(1024)(128)(2,1)} %param.19) | data formatting | bytes 8192 | tf_op jit(solution)/shard_map/broadcast_in_dim | solution.py:232
  32.4 9.5 %all-to-all-done.1.refs_1_ = bf16[16,4,2176]{2,1,0:T(4,128)(2,1)S(1)} async-done(((bf16[16,4,2176]{2,1,0:T(4,128)(2,1)}), bf16[16,4,2176]{2,1,0:T(4,128)(2,1)S(1)}, u32[]{:S(2)}, u32[]{:S(2)}) %all-to-all-start.1) | async-done | bytes 278560 | tf_op jit(solution)/shard_map/all_to_all | solution.py:214
  41.9 0.0 copy-start.1
  41.9 0.7 %copy-done.1 = bf16[4,2048]{1,0:T(4,128)(2,1)S(1)} copy-done((bf16[4,2048]{1,0:T(4,128)(2,1)S(1)}, bf16[4,2048]{1,0:T(4,128)(2,1)}, u32[]{:S(2)}) %copy-start.1) | copy-done | bytes 16408
  42.7 0.0 copy-start.3
  42.7 0.7 %copy-done.3 = bf16[4,2048]{1,0:T(4,128)(2,1)S(1)} copy-done((bf16[4,2048]{1,0:T(4,128)(2,1)S(1)}, bf16[4,2048]{1,0:T(4,128)(2,1)}, u32[]{:S(2)}) %copy-start.3) | copy-done | bytes 16408
  43.4 15.4 %project.1 = bf16[4,8192]{1,0:T(4,128)(2,1)S(1)} custom-call(s32[1]{0:T(128)} %bitcast.refs_0_.tp_index, bf16[16,4,2176]{2,1,0:T(4,128)(2,1)S(1)} %all-to-all-done.1.refs_1_, bf16[4,2048]{1,0:T(4,128)(2,1)S(1)} %copy-done.1, bf16[4,2048]{1,0:T(4,128)(2,1)S(1)} %copy-done.3, bf16[2048,8192]{1,0:T(8,128)(2,1)} %refs_4_.1), custom_call_target="tpu_custom_call" | custom-call | tf_op jit(solution)/shard_map/project/pallas_call | solution.py:215
  58.8 5.8 %all-gather.1.pieces = bf16[4,4,8192]{2,1,0:T(4,128)(2,1)S(1)} all-gather(bf16[1,4,8192]{2,1,0:T(4,128)(2,1)S(1)} %bitcast.4), channel_id=2, replica_groups=mesh['groups'=2,'kvb'=4,'tp'=4] {'tp'}, dimensions={0}, use_global_device_ids=true | all-gather | bytes 327680 | tf_op jit(solution)/shard_map/all_gather | solution.py:223
  64.6 0.0 copy-done.2
  64.6 0.8 %finish.1 = (bf16[4,2048]{1,0:T(4,128)(2,1)}, bf16[4,2048]{1,0:T(4,128)(2,1)}) custom-call(s32[1]{0:T(128)} %bitcast.refs_0_.tp_index, bf16[4,4,8192]{2,1,0:T(4,128)(2,1)S(1)} %all-gather.1.pieces, bf16[4,8192]{1,0:T(4,128)(2,1)S(1)} %copy-done.2, bf16[1,2048]{1,0:T(2,128)(2,1)S(1)} %broadcast_in_dim.18.gain), custom_call_target="tpu_custom_call" | custom-call | tf_op jit(solution)/shard_map/finish/pallas_call | solution.py:225
Async XLA Ops:
  0.6 64.0 %copy-start.2 = (bf16[4,8192]{1,0:T(4,128)(2,1)S(1)}, bf16[4,8192]{1,0:T(4,128)(2,1)}, u32[]{:S(2)}) copy-start(bf16[4,8192]{1,0:T(4,128)(2,1)} %residual.1) | copy-start | bytes 196612
  2.2 17.4 %all-to-all-start = ((bf16[16,4,2048]{2,1,0:T(4,128)(2,1)}), bf16[16,4,2048]{2,1,0:T(4,128)(2,1)S(1)}, u32[]{:S(2)}, u32[]{:S(2)}) async-start(bf16[16,4,2048]{2,1,0:T(4,128)(2,1)} %broadcast_in_dim.17), calls=%async_computation | async-start | bytes 524288 | tf_op jit(solution)/shard_map/all_to_all | solution.py:198
  19.6 2.2 %copy-start = (bf16[64,16,2048]{2,1,0:T(8,128)(2,1)S(1)}, bf16[64,16,2048]{2,1,0:T(8,128)(2,1)}, u32[]{:S(2)}) copy-start(bf16[64,16,2048]{2,1,0:T(8,128)(2,1)} %refs_5_.1) | copy-start | bytes 12582916
  21.8 0.7 %copy-start.4 = (s32[16]{0:T(128)S(1)}, s32[16]{0:T(128)}, u32[]{:S(2)}) copy-start(s32[16]{0:T(128)} %refs_0_.1) | copy-start | bytes 196
  22.5 0.7 %copy-start.5 = (s32[64]{0:T(128)S(1)}, s32[64]{0:T(128)}, u32[]{:S(2)}) copy-start(s32[64]{0:T(128)} %param.15) | copy-start | bytes 772
  23.1 0.7 %copy-start.6 = (s32[64]{0:T(128)S(1)}, s32[64]{0:T(128)}, u32[]{:S(2)}) copy-start(s32[64]{0:T(128)} %param.16) | copy-start | bytes 772
  28.2 13.8 %all-to-all-start.1 = ((bf16[16,4,2176]{2,1,0:T(4,128)(2,1)}), bf16[16,4,2176]{2,1,0:T(4,128)(2,1)S(1)}, u32[]{:S(2)}, u32[]{:S(2)}) async-start(bf16[16,4,2176]{2,1,0:T(4,128)(2,1)} %attend.1), calls=%async_computation.1 | async-start | bytes 557056 | tf_op jit(solution)/shard_map/all_to_all | solution.py:214
  41.9 0.7 %copy-start.1 = (bf16[4,2048]{1,0:T(4,128)(2,1)S(1)}, bf16[4,2048]{1,0:T(4,128)(2,1)}, u32[]{:S(2)}) copy-start(bf16[4,2048]{1,0:T(4,128)(2,1)} %refs_2_.1) | copy-start | bytes 49156
  42.7 0.7 %copy-start.3 = (bf16[4,2048]{1,0:T(4,128)(2,1)S(1)}, bf16[4,2048]{1,0:T(4,128)(2,1)}, u32[]{:S(2)}) copy-start(bf16[4,2048]{1,0:T(4,128)(2,1)} %refs_3_.1) | copy-start | bytes 49156
